TPU v7x, 32 devices: a whole 2x2x4 slice. The times are simulated.
32 devices in a mesh: dp: 2 (over x), tp: 16 (over y, z, core).
Axes of the slice: x: 2, y: 2, z: 4, core: 2. Of those that a mesh axis runs over, the one named last changes fastest.
Arguments:
- x: bfloat16 [4096, 8192], P(('dp', 'tp')), parts along dimension 0
- w_gate: bfloat16 [8192, 32768], P(None, 'tp')
- w_up: bfloat16 [8192, 32768], P(None, 'tp')
- w_down: bfloat16 [32768, 8192], P('tp')
Outputs:
- output: bfloat16 [4096, 8192], P(('dp', 'tp')), parts along dimension 0
There are 2 independent parts. A program takes and returns all parts, laid end to end along the dimension named above; an argument that names none is the same for every part.
All inputs are finite; a program needn't handle non-finite values.
Results may differ from a plain program's by a relative error of at most 0.016.
Values are sent between devices in bfloat16 or wider.
A program may use at most 2 GiB of HBM per device.

v0:
```python
import jax
import jax.numpy as jnp
from jax import lax
from jax.sharding import PartitionSpec as P


def solution(mesh):
    def step(x, w_gate, w_up, w_down):
        rows = lax.all_gather(x, "tp", axis=0, tiled=True)
        gate = jnp.dot(rows, w_gate, preferred_element_type=jnp.float32)
        up = jnp.dot(rows, w_up, preferred_element_type=jnp.float32)
        hidden = (jax.nn.silu(gate) * up).astype(jnp.bfloat16)
        term = jnp.dot(hidden, w_down, preferred_element_type=jnp.float32).astype(jnp.bfloat16)
        return lax.psum_scatter(term, "tp", scatter_dimension=0, tiled=True)

    return jax.shard_map(
        step,
        mesh=mesh,
        in_specs=(P(("dp", "tp"), None), P(None, "tp"), P(None, "tp"), P("tp", None)),
        out_specs=P(("dp", "tp"), None),
        check_vma=False,
    )
```

profile of v0, /device:TPU:0, one launch (start us, length us, event | category | flops | bytes accessed | tf_op | source)
XLA Modules:
  0.0 754.9 jit_solution(9000282202761011970)
XLA Ops:
  6.5 0.0 all-gather.2.cloned.1.call-start
  6.5 0.7 all-gather.2.cloned.1.call-update
  7.3 0.0 reduce-scatter.2.cloned.1.call-start
  7.3 172.3 %all-gather.2.cloned.1.call-done = bf16[2048,8192]{1,0:T(8,128)(2,1)} async-done(((bf16[128,8192]{1,0:T(8,128)(2,1)}), bf16[2048,8192]{1,0:T(8,128)(2,1)}) %all-gather.2.cloned.1.call-update) | async-done | bytes 33554448 | tf_op jit(solution)/shard_map/all_gather | solution.py:9
  179.7 79.1 %fusion = f32[2048,2048]{1,0:T(8,128)} fusion(bf16[2048,8192]{1,0:T(8,128)(2,1)} %all-gather.2.cloned.1.call-done, bf16[8192,2048]{1,0:T(8,128)(2,1)} %param.5), kind=kOutput, calls=%fused_computation.2 | convolution fusion | flops 68719476736 | bytes 83886080 | tf_op jit(solution)/shard_map/dot_general | solution.py:10
  258.7 83.1 %multiply_convert_fusion = bf16[2048,2048]{1,0:T(8,128)(2,1)} fusion(f32[2048,2048]{1,0:T(8,128)} %fusion, bf16[2048,8192]{1,0:T(8,128)(2,1)} %all-gather.2.cloned.1.call-done, bf16[8192,2048]{1,0:T(8,128)(2,1)} %param.6), kind=kOutput, calls=%fused_computation.1 | convolution fusion | flops 68744642560 | bytes 92274688 | tf_op jit(solution)/shard_map/dot_general | solution.py:11
  341.9 77.8 %convolution_convert_fusion = bf16[2048,8192]{1,0:T(8,128)(2,1)} fusion(bf16[2048,2048]{1,0:T(8,128)(2,1)} %multiply_convert_fusion, bf16[2048,8192]{1,0:T(8,128)(2,1)} %param.7), kind=kOutput, calls=%fused_computation | convolution fusion | flops 68736253952 | bytes 75497472 | tf_op jit(solution)/shard_map/dot_general | solution.py:13
  419.7 0.0 reduce-scatter.2.cloned.1.call-update
  419.7 328.3 %reduce-scatter.2.cloned.1.call-done = bf16[128,8192]{1,0:T(8,128)(2,1)} async-done(((bf16[2048,8192]{1,0:T(8,128)(2,1)}), bf16[128,8192]{1,0:T(8,128)(2,1)}) %reduce-scatter.2.cloned.1.call-update) | async-done | bytes 2097168 | tf_op jit(solution)/shard_map/reduce_scatter | solution.py:14
Async XLA Ops:
  6.5 173.1 %all-gather.2.cloned.1.call-start = ((), (), s32[]{:S(2)}) async-start(), calls=%async_computation.1 | async-start | bytes 35651584 | tf_op jit(solution)/shard_map/all_gather | solution.py:9
  7.3 740.8 %reduce-scatter.2.cloned.1.call-start = ((), (), s32[]{:S(2)}) async-start(), calls=%async_computation.2 | async-start | bytes 35651584 | tf_op jit(solution)/shard_map/reduce_scatter | solution.py:14
Sparse Core Ops, SparseCore 0:
  8.9 170.6 all-gather.1
  419.8 328.1 reduce-scatter.1
where the time goes:
time: 755 us
  waiting for transfers between devices  501 us (66%)
  matrix products  240 us (32%)
  between operations  13.4 us (2%)
    reduce_scatter x1, waiting for transfers between devices, step(): return lax.psum_scatter(term, 'tp', scatter_dimension=0, tiled=True)  328 us
    all_gather x1, waiting for transfers between devices, step(): rows = lax.all_gather(x, 'tp', axis=0, tiled=True)  172 us
    dot_general x1, matrix products, step(): up = jnp.dot(rows, w_up, preferred_element_type=jnp.float32)  83.1 us
    dot_general x1, matrix products, step(): gate = jnp.dot(rows, w_gate, preferred_element_type=jnp.float32)  79.1 us
    dot_general x1, matrix products, step(): jnp.dot(hidden, w_down, preferred_element_type=jnp.float32)  77.8 us
  transfers between devices with their start and end apart: 2, of which 2 were waited for; matrix products, arithmetic and copies ran while one was open for 0% of the time, Pallas kernels for 0%

commit v1 on v0

v1 whole, which is shorter than its diff:
```python
import functools

import jax
import jax.numpy as jnp
from jax import lax
from jax.experimental import pallas as pl
from jax.experimental.pallas import tpu as pltpu
from jax.sharding import PartitionSpec as P

MESH = pl.DeviceIdType.MESH
CHIPS = 8
TILES = 8
AGS_AT = 1
XL_AT = 6


def place():
    me = lax.axis_index("tp")
    core, chip = lax.rem(me, 2), lax.div(me, 2)
    y, z = lax.div(chip, 4), lax.rem(chip, 4)
    position = y * z + (1 - y) * (7 - z)

    def device(q):
        upper = lax.div(q, 4)
        return ((1 - upper) * (4 + q) + upper * (7 - q)) * 2 + core

    right = device(lax.rem(position + 1, CHIPS))
    left = device(lax.rem(position + CHIPS - 1, CHIPS))
    return core, right, left, chip * 2 + 1 - core


def kernel(
    x_ref, wg_ref, wu_ref, wd_ref, y_ref, xg_ref,
    xv, wgu, wdv, hid, acc, sib_out, sib_in, ring_out, ring_in, yv,
    x_sem, gu_sem, d_sem, ag_send, ag_recv, sx_send, sx_recv, so_send, so_recv, ro_send, ro_recv, y_sem,
):
    core, right, left, sib = place()
    mine = x_ref.shape[0]
    half = mine // 2
    tf, td = wgu.shape[3], wdv.shape[2]

    def remote(src, dst, send, recv, device):
        return pltpu.make_async_remote_copy(
            src_ref=src, dst_ref=dst, send_sem=send, recv_sem=recv, device_id={"tp": device}, device_id_type=MESH
        )

    def ag(src, k, way):
        rows = pl.ds(way * half, half)
        s = x_ref.at[rows] if src is None else xg_ref.at[src, core, rows]
        return remote(s, xg_ref.at[k + 1, core, rows], ag_send.at[k, way], ag_recv.at[k, way], (right, left)[way])

    def sx(src, k):
        s = x_ref if src is None else xg_ref.at[src, core]
        return remote(s, xg_ref.at[k, core], sx_send.at[k], sx_recv.at[k], sib)

    def load_mine(k):
        s = x_ref if k is None else xg_ref.at[k, core]
        return pltpu.make_async_copy(s, xv.at[pl.ds(0, mine)], x_sem.at[0])

    def load_other(k):
        return pltpu.make_async_copy(xg_ref.at[k, 1 - core], xv.at[pl.ds(mine, mine)], x_sem.at[1])

    def gu(j, slot):
        columns = pl.ds(pl.multiple_of(j * tf, tf), tf)
        return (
            pltpu.make_async_copy(wg_ref.at[:, columns], wgu.at[slot, 0], gu_sem.at[slot, 0]),
            pltpu.make_async_copy(wu_ref.at[:, columns], wgu.at[slot, 1], gu_sem.at[slot, 1]),
        )

    def start_gu(j, slot):
        for c in gu(j, slot):
            c.start()

    def down(n, slot):
        columns = pl.ds(pl.multiple_of(n * td, td), td)
        return pltpu.make_async_copy(wd_ref.at[:, columns], wdv.at[slot], d_sem.at[slot])

    def to_sib(parity, n):
        return remote(
            sib_out.at[lax.rem(n, 2)], sib_in.at[parity, n], so_send.at[lax.rem(n, 2)], so_recv.at[parity, n], sib
        )

    def to_ring(k, m, way):
        rows = pl.ds(way * half, half)
        return remote(
            ring_out.at[lax.rem(m, 2), rows],
            ring_in.at[k, m, rows],
            ro_send.at[lax.rem(m, 2), way],
            ro_recv.at[k, m, way],
            (right, left)[way],
        )

    def project(slot, more):
        def tile(j, _):
            now = lax.rem(j, 2)

            def ahead():
                start_gu(lax.rem(j + 1, TILES), 1 - now)

            if more:
                ahead()
            else:
                pl.when(j < TILES - 1)(ahead)
            for c in gu(j, now):
                c.wait()
            gate = jnp.dot(xv[...], wgu[now, 0], preferred_element_type=jnp.float32)
            up = jnp.dot(xv[...], wgu[now, 1], preferred_element_type=jnp.float32)
            columns = pl.ds(pl.multiple_of(j * tf, tf), tf)
            hid[slot, :, columns] = (jax.nn.silu(gate) * up).astype(jnp.bfloat16)
            return 0

        lax.fori_loop(0, TILES, tile, 0)

    def arrive(k):
        for way in range(2):
            ag(0, k - 1, way).wait_recv()

            @pl.when(k < CHIPS - 1)
            def _():
                ag(k, k, way).start()

        sx(k, k).start()

    def fetch(k):
        sx(k, k).wait_recv()
        load_mine(k).start()
        load_other(k).start()

    def sums(k, last):
        slot = 0 if last else 1
        parity = lax.rem(k, 2)

        def tile(n, _):
            now = lax.rem(n, 2)

            @pl.when(n < TILES)
            def _():
                if last:
                    pl.when(n < TILES - 1)(lambda: down(n + 1, 1 - now).start())
                else:
                    pl.when((n < TILES - 1) | (k == CHIPS - 1))(
                        lambda: down(lax.rem(n + 1, TILES), 1 - now).start()
                    )
                down(n, now).wait()
                term = jnp.dot(hid[slot], wdv[now], preferred_element_type=jnp.float32)
                acc[now] = term[:mine]
                if last:
                    to_sib(parity, n).wait_send()
                else:
                    pl.when((k > 1) | (n >= 2))(lambda: to_sib(parity, n).wait_send())
                sib_out[now] = term[mine:].astype(jnp.bfloat16)
                to_sib(parity, n).start()

            if not last:

                @pl.when((n == AGS_AT) & (k < CHIPS - 1))
                def _():
                    arrive(k + 1)

                @pl.when((n == XL_AT) & (k < CHIPS - 1))
                def _():
                    fetch(k + 1)

            @pl.when(n >= 1)
            def _():
                m = n - 1
                then = 1 - now
                to_sib(parity, m).wait_recv()
                if last:
                    for way in range(2):
                        to_ring(k - 1, m, way).wait_recv()
                    pl.when(m >= 2)(lambda: out(m).wait())
                    total = acc[then] + sib_in[parity, m].astype(jnp.float32)
                    total = total + ring_in[k - 1, m].astype(jnp.float32)
                    yv[then] = total.astype(jnp.bfloat16)
                    out(m).start()
                else:

                    @pl.when((k > 1) | (m >= 2))
                    def _():
                        for way in range(2):
                            to_ring(k, m, way).wait_send()

                    @pl.when(k == 1)
                    def _():
                        total = acc[then] + sib_in[parity, m].astype(jnp.float32)
                        ring_out[then] = total.astype(jnp.bfloat16)

                    @pl.when(k > 1)
                    def _():
                        for way in range(2):
                            to_ring(k - 1, m, way).wait_recv()
                        total = acc[then] + sib_in[parity, m].astype(jnp.float32)
                        total = total + ring_in[k - 1, m].astype(jnp.float32)
                        ring_out[then] = total.astype(jnp.bfloat16)

                    for way in range(2):
                        to_ring(k, m, way).start()

            return 0

        lax.fori_loop(0, TILES + 1, tile, 0)

    def out(m):
        columns = pl.ds(pl.multiple_of(m * td, td), td)
        return pltpu.make_async_copy(yv.at[lax.rem(m, 2)], y_ref.at[:, columns], y_sem.at[lax.rem(m, 2)])

    start_gu(0, 0)
    load_mine(None).start()
    barrier = pltpu.get_barrier_semaphore()
    for partner in (left, right, sib):
        pl.semaphore_signal(barrier, inc=1, device_id={"tp": partner}, device_id_type=MESH)
    pl.semaphore_wait(barrier, 3)

    sx(None, 0).start()
    for way in range(2):
        ag(None, 0, way).start()
    sx(None, 0).wait_recv()
    load_other(0).start()
    load_mine(None).wait()
    load_other(0).wait()
    project(0, True)
    arrive(1)
    fetch(1)

    def step(k, _):
        down(0, 0).start()
        load_mine(k).wait()
        load_other(k).wait()
        project(1, False)
        pl.when(k < CHIPS - 1)(lambda: start_gu(0, 0))
        sums(k, False)
        return 0

    lax.fori_loop(1, CHIPS, step, 0)
    sums(CHIPS, True)

    for n in range(2):
        to_sib(0, n).wait_send()
        for way in range(2):
            to_ring(CHIPS - 1, n, way).wait_send()
        out(n).wait()

    def sent(k, _):
        sx(k, k).wait_send()
        return 0

    lax.fori_loop(0, CHIPS, sent, 0)

    def sent_on(k, _):
        for way in range(2):
            ag(k, k, way).wait_send()
        return 0

    lax.fori_loop(0, CHIPS - 1, sent_on, 0)


def block(x, w_gate, w_up, w_down):
    mine, d = x.shape
    f = w_gate.shape[1]
    tf, td = f // TILES, d // TILES
    bf16, dma = jnp.bfloat16, pltpu.SemaphoreType.DMA
    hbm = pl.BlockSpec(memory_space=pl.ANY)
    y, _ = pl.pallas_call(
        kernel,
        out_shape=(
            jax.ShapeDtypeStruct((mine, d), bf16),
            jax.ShapeDtypeStruct((CHIPS, 2, mine, d), bf16),
        ),
        in_specs=[hbm] * 4,
        out_specs=(hbm, hbm),
        scratch_shapes=[
            pltpu.VMEM((2 * mine, d), bf16),
            pltpu.VMEM((2, 2, d, tf), bf16),
            pltpu.VMEM((2, f, td), bf16),
            pltpu.VMEM((2, 2 * mine, f), bf16),
            pltpu.VMEM((2, mine, td), jnp.float32),
            pltpu.VMEM((2, mine, td), bf16),
            pltpu.VMEM((2, TILES, mine, td), bf16),
            pltpu.VMEM((2, mine, td), bf16),
            pltpu.VMEM((CHIPS, TILES, mine, td), bf16),
            pltpu.VMEM((2, mine, td), bf16),
            dma((2,)),
            dma((2, 2)),
            dma((2,)),
            dma((CHIPS - 1, 2)),
            dma((CHIPS - 1, 2)),
            dma((CHIPS,)),
            dma((CHIPS,)),
            dma((2,)),
            dma((2, TILES)),
            dma((2, 2)),
            dma((CHIPS, TILES, 2)),
            dma((2,)),
        ],
        compiler_params=pltpu.CompilerParams(
            collective_id=0, has_side_effects=True, vmem_limit_bytes=67_043_328
        ),
        cost_estimate=pl.CostEstimate(
            flops=6 * CHIPS * 2 * mine * d * f,
            bytes_accessed=CHIPS * 6 * d * f,
            transcendentals=CHIPS * 2 * mine * f,
        ),
    )(x, w_gate, w_up, w_down)
    return y


def solution(mesh):
    return jax.shard_map(
        block,
        mesh=mesh,
        in_specs=(P(("dp", "tp"), None), P(None, "tp"), P(None, "tp"), P("tp", None)),
        out_specs=P(("dp", "tp"), None),
        check_vma=False,
    )
```

time: 755 us -> 502 us (0.66)
  waiting for transfers between devices: 501 us -> 0 us
  Pallas kernels: 0 us -> 498 us
  matrix products: 240 us -> 0 us
  between operations: 13.4 us -> 0.01 us
    pallas_call x0 -> x1, Pallas kernels: none -> 498 us  [block(): pl.pallas_call(kernel, out_shape=(jax.ShapeDtypeStruct((mine, d), bf16),...]
    reduce_scatter x1 -> x0, waiting for transfers between devices: 328 us -> none  [step(): return lax.psum_scatter(term, 'tp', scatter_dimension=0, tiled=True)]
    dot_general x3 -> x0, matrix products: 240 us -> none  [the longest x1 83.1 us: step(): up = jnp.dot(rows, w_up, preferred_element_type=jnp.float32)]
    all_gather x1 -> x0, waiting for transfers between devices: 172 us -> none  [step(): rows = lax.all_gather(x, 'tp', axis=0, tiled=True)]
  transfers between devices with their start and end apart: 2 -> 0, of which waited for: 2 -> 0; matrix products, arithmetic and copies ran while one was open for 0% -> 0% of each run, Pallas kernels for 0% -> 0%
where the time goes in v1:
time: 502 us; the launch traced here: 501 us
  Pallas kernels  498 us (99%)
    pallas_call x1, Pallas kernels, block(): pl.pallas_call(kernel, out_shape=(jax.ShapeDtypeStruct((mine, d), bf16),...  498 us

profile of v1, /device:TPU:0, one launch (start us, length us, event | category | flops | bytes accessed | tf_op | source)
XLA Modules:
  0.0 500.7 jit_solution(14852945339786349576)
XLA Ops:
  0.0 497.6 %shard_map.46 = (bf16[128,8192]{1,0:T(8,128)(2,1)}, bf16[8,2,128,8192]{3,2,1,0:T(8,128)(2,1)}) custom-call(bf16[128,8192]{1,0:T(8,128)(2,1)} %x_ref.1, bf16[8192,2048]{1,0:T(8,128)(2,1)} %wg_ref.1, bf16[8192,2048]{1,0:T(8,128)(2,1)} %wu_ref.1, bf16[2048,8192]{1,0:T(8,128)(2,1)} %wd_ref.1), custom_call_target="tpu_custom_call" | custom-call | flops 206158430208 | bytes 805306368 | tf_op jit(solution)/shard_map/pallas_call | solution.py:264
  497.6 3.1 copy.6

commit v2 on v1

v2 whole, which is shorter than its diff:
```python
import functools

import jax
import jax.numpy as jnp
from jax import lax
from jax.experimental import pallas as pl
from jax.experimental.pallas import tpu as pltpu
from jax.sharding import PartitionSpec as P

MESH = pl.DeviceIdType.MESH
CHIPS = 8
TILES = 8
PIECES = 4
SLOTS = 7
LAG = 2
XL_AT = 2
FIRST = 2 * TILES
STEP = 3 * TILES
LAST = FIRST + (CHIPS - 1) * STEP


def place():
    me = lax.axis_index("tp")
    core, chip = lax.rem(me, 2), lax.div(me, 2)
    y, z = lax.div(chip, 4), lax.rem(chip, 4)
    position = y * z + (1 - y) * (7 - z)

    def device(q):
        upper = lax.div(q, 4)
        return ((1 - upper) * (4 + q) + upper * (7 - q)) * 2 + core

    right = device(lax.rem(position + 1, CHIPS))
    left = device(lax.rem(position + CHIPS - 1, CHIPS))
    return core, right, left, chip * 2 + 1 - core


def kernel(
    x_ref, wg_ref, wu_ref, wd_ref, y_ref, xg_ref,
    xv, w, hid, acc, sib_out, sib_in, ring_out, ring_in, yv,
    x_sem, w_sem, ag_send, ag_recv, sx_send, sx_recv, so_send, so_recv, ro_send, ro_recv, y_sem,
):
    core, right, left, sib = place()
    mine = x_ref.shape[0]
    half = mine // 2
    piece = half // PIECES
    f, tf = hid.shape[2], w.shape[2]
    td = acc.shape[2]
    parts = td // tf

    def remote(src, dst, send, recv, device):
        return pltpu.make_async_remote_copy(
            src_ref=src, dst_ref=dst, send_sem=send, recv_sem=recv, device_id={"tp": device}, device_id_type=MESH
        )

    def rows_of(way, p):
        return pl.ds(pl.multiple_of(way * half + p * piece, piece), piece)

    def ag(src, k, p, way):
        rows = rows_of(way, p)
        s = x_ref.at[rows] if src is None else xg_ref.at[src, core, rows]
        return remote(s, xg_ref.at[k + 1, core, rows], ag_send.at[k], ag_recv.at[k, p, way], (right, left)[way])

    def sx(src, k, rows):
        s = x_ref.at[rows] if src is None else xg_ref.at[src, core, rows]
        return remote(s, xg_ref.at[k, core, rows], sx_send.at[k], sx_recv.at[k], sib)

    everything = pl.ds(0, mine)

    def load_mine(k):
        s = x_ref if k is None else xg_ref.at[k, core]
        return pltpu.make_async_copy(s, xv.at[pl.ds(0, mine)], x_sem.at[0])

    def load_other(k):
        return pltpu.make_async_copy(xg_ref.at[k, 1 - core], xv.at[pl.ds(mine, mine)], x_sem.at[1])

    def start_weights(i):
        slot = lax.rem(i, SLOTS)
        r = i - FIRST
        q = jnp.where(i < FIRST, i, jnp.where(i < LAST, lax.rem(r, STEP), i - LAST + FIRST))

        def columns(j):
            return pl.ds(pl.multiple_of(j * tf, tf), tf)

        @pl.when((q < FIRST) & (lax.rem(q, 2) == 0))
        def _():
            pltpu.make_async_copy(wg_ref.at[:, columns(lax.div(q, 2))], w.at[slot], w_sem.at[slot]).start()

        @pl.when((q < FIRST) & (lax.rem(q, 2) == 1))
        def _():
            pltpu.make_async_copy(wu_ref.at[:, columns(lax.div(q, 2))], w.at[slot], w_sem.at[slot]).start()

        @pl.when((q >= FIRST) & (i < LAST + TILES))
        def _():
            for part in range(parts):
                pltpu.make_async_copy(
                    wd_ref.at[:, columns((q - FIRST) * parts + part)],
                    w.at[slot, pl.ds(part * f, f)],
                    w_sem.at[slot],
                ).start()

    def wait_weights(i):
        slot = lax.rem(i, SLOTS)
        pltpu.make_async_copy(wg_ref.at[:, pl.ds(0, tf)], w.at[slot], w_sem.at[slot]).wait()
        return slot

    def to_sib(parity, n):
        t = lax.rem(n, LAG + 1)
        return remote(sib_out.at[t], sib_in.at[parity, n], so_send.at[t], so_recv.at[parity, n], sib)

    def to_ring(k, m, way):
        rows = pl.ds(way * half, half)
        return remote(
            ring_out.at[m, rows], ring_in.at[k, m, rows], ro_send.at[m, way], ro_recv.at[k, m, way], (right, left)[way]
        )

    def arrive(k, p):
        for way in range(2):
            ag(0, k - 1, p, way).wait_recv()

            @pl.when(k < CHIPS - 1)
            def _():
                ag(k, k, p, way).start()

            sx(k, k, rows_of(way, p)).start()

    def fetch(k):
        sx(k, k, everything).wait_recv()
        load_mine(k).start()
        load_other(k).start()

    def project(slot, item, k):
        def tile(j, _):
            i = item + 2 * j
            start_weights(i + SLOTS - 2)
            start_weights(i + SLOTS - 1)
            g = wait_weights(i)
            u = wait_weights(i + 1)
            gate = jnp.dot(xv[...], w[g], preferred_element_type=jnp.float32)
            up = jnp.dot(xv[...], w[u], preferred_element_type=jnp.float32)
            columns = pl.ds(pl.multiple_of(j * tf, tf), tf)
            hid[slot, :, columns] = (jax.nn.silu(gate) * up).astype(jnp.bfloat16)

            @pl.when((lax.rem(j, TILES // PIECES) == TILES // PIECES - 1) & (k < CHIPS))
            def _():
                arrive(k, lax.div(j, TILES // PIECES))

            return 0

        lax.fori_loop(0, TILES, tile, 0)

    def sums(k, item, last):
        slot = 0 if last else 1
        parity = lax.rem(k, 2)

        def tile(n, _):
            @pl.when(n < TILES)
            def _():
                now = lax.rem(n, LAG + 1)
                i = item + n
                start_weights(i + SLOTS - 2)
                v = wait_weights(i)
                if last:
                    to_sib(parity, n).wait_send()
                else:
                    pl.when((k > 1) | (n >= LAG + 1))(lambda: to_sib(parity, n).wait_send())
                for part in range(parts):
                    term = jnp.dot(hid[slot], w[v, part * f : (part + 1) * f], preferred_element_type=jnp.float32)
                    acc[now, :, part * tf : (part + 1) * tf] = term[:mine]
                    sib_out[now, :, part * tf : (part + 1) * tf] = term[mine:].astype(jnp.bfloat16)
                to_sib(parity, n).start()

            if not last:

                @pl.when((n == XL_AT) & (k < CHIPS - 1))
                def _():
                    fetch(k + 1)

            @pl.when(n >= LAG)
            def _():
                m = n - LAG
                then = lax.rem(m, LAG + 1)
                t = lax.rem(m, 2)
                to_sib(parity, m).wait_recv()
                if last:
                    for way in range(2):
                        to_ring(k - 1, m, way).wait_recv()
                    pl.when(m >= 2)(lambda: out(m).wait())
                    total = acc[then] + sib_in[parity, m].astype(jnp.float32)
                    total = total + ring_in[k - 1, m].astype(jnp.float32)
                    yv[t] = total.astype(jnp.bfloat16)
                    out(m).start()
                else:

                    @pl.when(k > 1)
                    def _():
                        for way in range(2):
                            to_ring(k, m, way).wait_send()

                    @pl.when(k == 1)
                    def _():
                        total = acc[then] + sib_in[parity, m].astype(jnp.float32)
                        ring_out[m] = total.astype(jnp.bfloat16)

                    @pl.when(k > 1)
                    def _():
                        for way in range(2):
                            to_ring(k - 1, m, way).wait_recv()
                        total = acc[then] + sib_in[parity, m].astype(jnp.float32)
                        total = total + ring_in[k - 1, m].astype(jnp.float32)
                        ring_out[m] = total.astype(jnp.bfloat16)

                    for way in range(2):
                        to_ring(k, m, way).start()

            return 0

        lax.fori_loop(0, TILES + LAG, tile, 0)

    def out(m):
        columns = pl.ds(pl.multiple_of(m * td, td), td)
        return pltpu.make_async_copy(yv.at[lax.rem(m, 2)], y_ref.at[:, columns], y_sem.at[lax.rem(m, 2)])

    load_mine(None).start()
    for i in range(SLOTS - 2):
        start_weights(jnp.int32(i))
    barrier = pltpu.get_barrier_semaphore()
    for partner in (left, right, sib):
        pl.semaphore_signal(barrier, inc=1, device_id={"tp": partner}, device_id_type=MESH)
    pl.semaphore_wait(barrier, 3)

    sx(None, 0, everything).start()
    for p in range(PIECES):
        for way in range(2):
            ag(None, 0, p, way).start()
    sx(None, 0, everything).wait_recv()
    load_other(0).start()
    load_mine(None).wait()
    load_other(0).wait()
    project(0, 0, 1)
    fetch(1)

    def step(k, _):
        item = FIRST + (k - 1) * STEP
        load_mine(k).wait()
        load_other(k).wait()
        project(1, item, k + 1)
        sums(k, item + FIRST, False)
        return 0

    lax.fori_loop(1, CHIPS, step, 0)
    sums(CHIPS, LAST, True)

    for n in range(LAG + 1):
        to_sib(0, n).wait_send()
    for n in range(2):
        out(n).wait()

    def summed(m, _):
        for way in range(2):
            to_ring(CHIPS - 1, m, way).wait_send()
        return 0

    lax.fori_loop(0, TILES, summed, 0)

    def sent(k, _):
        sx(k, k, everything).wait_send()
        return 0

    lax.fori_loop(0, CHIPS, sent, 0)

    def sent_on(k, _):
        remote(x_ref, xg_ref.at[k, core], ag_send.at[k], sx_recv.at[k], sib).wait_send()
        return 0

    lax.fori_loop(0, CHIPS - 1, sent_on, 0)


def block(x, w_gate, w_up, w_down):
    mine, d = x.shape
    f = w_gate.shape[1]
    tf, td = f // TILES, d // TILES
    bf16, dma = jnp.bfloat16, pltpu.SemaphoreType.DMA
    hbm = pl.BlockSpec(memory_space=pl.ANY)
    y, _ = pl.pallas_call(
        kernel,
        out_shape=(
            jax.ShapeDtypeStruct((mine, d), bf16),
            jax.ShapeDtypeStruct((CHIPS, 2, mine, d), bf16),
        ),
        in_specs=[hbm] * 4,
        out_specs=(hbm, hbm),
        scratch_shapes=[
            pltpu.VMEM((2 * mine, d), bf16),
            pltpu.VMEM((SLOTS, d, tf), bf16),
            pltpu.VMEM((2, 2 * mine, f), bf16),
            pltpu.VMEM((LAG + 1, mine, td), jnp.float32),
            pltpu.VMEM((LAG + 1, mine, td), bf16),
            pltpu.VMEM((2, TILES, mine, td), bf16),
            pltpu.VMEM((TILES, mine, td), bf16),
            pltpu.VMEM((CHIPS, TILES, mine, td), bf16),
            pltpu.VMEM((2, mine, td), bf16),
            dma((2,)),
            dma((SLOTS,)),
            dma((CHIPS - 1,)),
            dma((CHIPS - 1, PIECES, 2)),
            dma((CHIPS,)),
            dma((CHIPS,)),
            dma((LAG + 1,)),
            dma((2, TILES)),
            dma((TILES, 2)),
            dma((CHIPS, TILES, 2)),
            dma((2,)),
        ],
        compiler_params=pltpu.CompilerParams(
            collective_id=0, has_side_effects=True, vmem_limit_bytes=67_043_328
        ),
        cost_estimate=pl.CostEstimate(
            flops=6 * CHIPS * 2 * mine * d * f,
            bytes_accessed=CHIPS * 6 * d * f,
            transcendentals=CHIPS * 2 * mine * f,
        ),
    )(x, w_gate, w_up, w_down)
    return y


def solution(mesh):
    return jax.shard_map(
        block,
        mesh=mesh,
        in_specs=(P(("dp", "tp"), None), P(None, "tp"), P(None, "tp"), P("tp", None)),
        out_specs=P(("dp", "tp"), None),
        check_vma=False,
    )
```

time: 502 us -> 330 us (0.66)
  Pallas kernels: 498 us -> 327 us
    pallas_call x1, Pallas kernels: 498 us -> 327 us  [block(): pl.pallas_call(kernel, out_shape=(jax.ShapeDtypeStruct((mine, d), bf16),...]
where the time goes in v2:
time: 330 us
  Pallas kernels  327 us (99%)
    pallas_call x1, Pallas kernels, block(): pl.pallas_call(kernel, out_shape=(jax.ShapeDtypeStruct((mine, d), bf16),...  327 us

profile of v2, /device:TPU:0, one launch (start us, length us, event | category | flops | bytes accessed | tf_op | source)
XLA Modules:
  0.0 329.7 jit_solution(10705312616788588393)
XLA Ops:
  0.0 326.6 %shard_map.46 = (bf16[128,8192]{1,0:T(8,128)(2,1)}, bf16[8,2,128,8192]{3,2,1,0:T(8,128)(2,1)}) custom-call(bf16[128,8192]{1,0:T(8,128)(2,1)} %x_ref.1, bf16[8192,2048]{1,0:T(8,128)(2,1)} %wg_ref.1, bf16[8192,2048]{1,0:T(8,128)(2,1)} %wu_ref.1, bf16[2048,8192]{1,0:T(8,128)(2,1)} %wd_ref.1), custom_call_target="tpu_custom_call" | custom-call | flops 206158430208 | bytes 805306368 | tf_op jit(solution)/shard_map/pallas_call | solution.py:284
  326.6 3.1 copy.6

commit v3 on v2

--- a/solution.py
+++ b/solution.py
@@ -11,7 +11,7 @@
 CHIPS = 8
 TILES = 8
 PIECES = 4
-SLOTS = 7
+SLOTS = 6
 LAG = 2
 XL_AT = 2
 FIRST = 2 * TILES
@@ -104,13 +104,16 @@
         return slot
 
     def to_sib(parity, n):
-        t = lax.rem(n, LAG + 1)
-        return remote(sib_out.at[t], sib_in.at[parity, n], so_send.at[t], so_recv.at[parity, n], sib)
+        return remote(sib_out.at[n], sib_in.at[parity, n], so_send.at[n], so_recv.at[parity, n], sib)
 
     def to_ring(k, m, way):
         rows = pl.ds(way * half, half)
         return remote(
-            ring_out.at[m, rows], ring_in.at[k, m, rows], ro_send.at[m, way], ro_recv.at[k, m, way], (right, left)[way]
+            ring_out.at[m, rows],
+            ring_in.at[k - 1, m, rows],
+            ro_send.at[m, way],
+            ro_recv.at[k - 1, m, way],
+            (right, left)[way],
         )
 
     def arrive(k, p):
@@ -127,6 +130,34 @@
         sx(k, k, everything).wait_recv()
         load_mine(k).start()
         load_other(k).start()
+
+    def combine(k, m):
+        to_sib(lax.rem(k, 2), m).wait_recv()
+
+        @pl.when(k == 1)
+        def _():
+            ring_out[m] = (acc[m] + sib_in[lax.rem(k, 2), m].astype(jnp.float32)).astype(jnp.bfloat16)
+
+        @pl.when(k > 1)
+        def _():
+            for way in range(2):
+                to_ring(k - 1, m, way).wait_send()
+                to_ring(k - 1, m, way).wait_recv()
+            total = acc[m] + sib_in[lax.rem(k, 2), m].astype(jnp.float32)
+            ring_out[m] = (total + ring_in[k - 2, m].astype(jnp.float32)).astype(jnp.bfloat16)
+
+        for way in range(2):
+            to_ring(k, m, way).start()
+
+    def finish(m):
+        to_sib(0, m).wait_recv()
+        for way in range(2):
+            to_ring(CHIPS - 1, m, way).wait_recv()
+        t = lax.rem(m, 2)
+        pl.when(m >= 2)(lambda: out(m).wait())
+        total = acc[m] + sib_in[0, m].astype(jnp.float32)
+        yv[t] = (total + ring_in[CHIPS - 2, m].astype(jnp.float32)).astype(jnp.bfloat16)
+        out(m).start()
 
     def project(slot, item, k):
         def tile(j, _):
@@ -140,10 +171,12 @@
             columns = pl.ds(pl.multiple_of(j * tf, tf), tf)
             hid[slot, :, columns] = (jax.nn.silu(gate) * up).astype(jnp.bfloat16)
 
-            @pl.when((lax.rem(j, TILES // PIECES) == TILES // PIECES - 1) & (k < CHIPS))
+            @pl.when((lax.rem(j, TILES // PIECES) == TILES // PIECES - 1) & (k < CHIPS - 1))
             def _():
-                arrive(k, lax.div(j, TILES // PIECES))
-
+                arrive(k + 1, lax.div(j, TILES // PIECES))
+
+            if slot:
+                pl.when(k > 1)(lambda: combine(k - 1, j))
             return 0
 
         lax.fori_loop(0, TILES, tile, 0)
@@ -155,63 +188,24 @@
         def tile(n, _):
             @pl.when(n < TILES)
             def _():
-                now = lax.rem(n, LAG + 1)
                 i = item + n
                 start_weights(i + SLOTS - 2)
                 v = wait_weights(i)
                 if last:
                     to_sib(parity, n).wait_send()
                 else:
-                    pl.when((k > 1) | (n >= LAG + 1))(lambda: to_sib(parity, n).wait_send())
+                    pl.when(k > 1)(lambda: to_sib(parity, n).wait_send())
                 for part in range(parts):
                     term = jnp.dot(hid[slot], w[v, part * f : (part + 1) * f], preferred_element_type=jnp.float32)
-                    acc[now, :, part * tf : (part + 1) * tf] = term[:mine]
-                    sib_out[now, :, part * tf : (part + 1) * tf] = term[mine:].astype(jnp.bfloat16)
+                    acc[n, :, part * tf : (part + 1) * tf] = term[:mine]
+                    sib_out[n, :, part * tf : (part + 1) * tf] = term[mine:].astype(jnp.bfloat16)
                 to_sib(parity, n).start()
 
-            if not last:
-
-                @pl.when((n == XL_AT) & (k < CHIPS - 1))
-                def _():
-                    fetch(k + 1)
-
-            @pl.when(n >= LAG)
-            def _():
-                m = n - LAG
-                then = lax.rem(m, LAG + 1)
-                t = lax.rem(m, 2)
-                to_sib(parity, m).wait_recv()
-                if last:
-                    for way in range(2):
-                        to_ring(k - 1, m, way).wait_recv()
-                    pl.when(m >= 2)(lambda: out(m).wait())
-                    total = acc[then] + sib_in[parity, m].astype(jnp.float32)
-                    total = total + ring_in[k - 1, m].astype(jnp.float32)
-                    yv[t] = total.astype(jnp.bfloat16)
-                    out(m).start()
-                else:
-
-                    @pl.when(k > 1)
-                    def _():
-                        for way in range(2):
-                            to_ring(k, m, way).wait_send()
-
-                    @pl.when(k == 1)
-                    def _():
-                        total = acc[then] + sib_in[parity, m].astype(jnp.float32)
-                        ring_out[m] = total.astype(jnp.bfloat16)
-
-                    @pl.when(k > 1)
-                    def _():
-                        for way in range(2):
-                            to_ring(k - 1, m, way).wait_recv()
-                        total = acc[then] + sib_in[parity, m].astype(jnp.float32)
-                        total = total + ring_in[k - 1, m].astype(jnp.float32)
-                        ring_out[m] = total.astype(jnp.bfloat16)
-
-                    for way in range(2):
-                        to_ring(k, m, way).start()
-
+            if last:
+                pl.when(n >= LAG)(lambda: finish(n - LAG))
+            else:
+                pl.when((n == XL_AT) & (k < CHIPS - 1))(lambda: fetch(k + 1))
+                pl.when((n >= LAG) & (k == CHIPS - 1))(lambda: combine(k, n - LAG))
             return 0
 
         lax.fori_loop(0, TILES + LAG, tile, 0)
@@ -236,26 +230,25 @@
     load_other(0).start()
     load_mine(None).wait()
     load_other(0).wait()
-    project(0, 0, 1)
+    project(0, 0, 0)
     fetch(1)
 
     def step(k, _):
         item = FIRST + (k - 1) * STEP
         load_mine(k).wait()
         load_other(k).wait()
-        project(1, item, k + 1)
+        project(1, item, k)
         sums(k, item + FIRST, False)
         return 0
 
     lax.fori_loop(1, CHIPS, step, 0)
     sums(CHIPS, LAST, True)
 
-    for n in range(LAG + 1):
-        to_sib(0, n).wait_send()
     for n in range(2):
         out(n).wait()
 
     def summed(m, _):
+        to_sib(0, m).wait_send()
         for way in range(2):
             to_ring(CHIPS - 1, m, way).wait_send()
         return 0
@@ -293,11 +286,11 @@
             pltpu.VMEM((2 * mine, d), bf16),
             pltpu.VMEM((SLOTS, d, tf), bf16),
             pltpu.VMEM((2, 2 * mine, f), bf16),
-            pltpu.VMEM((LAG + 1, mine, td), jnp.float32),
-            pltpu.VMEM((LAG + 1, mine, td), bf16),
+            pltpu.VMEM((TILES, mine, td), jnp.float32),
+            pltpu.VMEM((TILES, mine, td), bf16),
             pltpu.VMEM((2, TILES, mine, td), bf16),
             pltpu.VMEM((TILES, mine, td), bf16),
-            pltpu.VMEM((CHIPS, TILES, mine, td), bf16),
+            pltpu.VMEM((CHIPS - 1, TILES, mine, td), bf16),
             pltpu.VMEM((2, mine, td), bf16),
             dma((2,)),
             dma((SLOTS,)),
@@ -305,10 +298,10 @@
             dma((CHIPS - 1, PIECES, 2)),
             dma((CHIPS,)),
             dma((CHIPS,)),
-            dma((LAG + 1,)),
+            dma((TILES,)),
             dma((2, TILES)),
             dma((TILES, 2)),
-            dma((CHIPS, TILES, 2)),
+            dma((CHIPS - 1, TILES, 2)),
             dma((2,)),
         ],
         compiler_params=pltpu.CompilerParams(

time: 330 us -> 326 us (0.988)
  Pallas kernels: 327 us -> 323 us
    pallas_call x1, Pallas kernels: 327 us -> 323 us  [block(): pl.pallas_call(kernel, out_shape=(jax.ShapeDtypeStruct((mine, d), bf16),...]
where the time goes in v3:
time: 326 us
  Pallas kernels  323 us (99%)
    pallas_call x1, Pallas kernels, block(): pl.pallas_call(kernel, out_shape=(jax.ShapeDtypeStruct((mine, d), bf16),...  323 us

profile of v3, /device:TPU:0, one launch (start us, length us, event | category | flops | bytes accessed | tf_op | source)
XLA Modules:
  0.0 325.9 jit_solution(18194577518110392575)
XLA Ops:
  0.0 322.8 %shard_map.46 = (bf16[128,8192]{1,0:T(8,128)(2,1)}, bf16[8,2,128,8192]{3,2,1,0:T(8,128)(2,1)}) custom-call(bf16[128,8192]{1,0:T(8,128)(2,1)} %x_ref.1, bf16[8192,2048]{1,0:T(8,128)(2,1)} %wg_ref.1, bf16[8192,2048]{1,0:T(8,128)(2,1)} %wu_ref.1, bf16[2048,8192]{1,0:T(8,128)(2,1)} %wd_ref.1), custom_call_target="tpu_custom_call" | custom-call | flops 206158430208 | bytes 805306368 | tf_op jit(solution)/shard_map/pallas_call | solution.py:277
  322.8 3.1 copy.6
